TPU v7x, 32 devices: a whole 2x2x4 slice. The times are simulated.
32 devices in a mesh: dp: 4 (over z), mp: 8 (over y, x, core).
Axes of the slice: x: 2, y: 2, z: 4, core: 2. Of those that a mesh axis runs over, the one named last changes fastest.
Arguments:
- policy_hidden: bfloat16 [256, 3584], P('dp'), may hold values from -96 to 96
- reference_hidden: bfloat16 [256, 3584], P('dp'), may hold values from -96 to 96
- policy_gain: float32 [3584], replicated, may hold values from 0.5 to 1.5
- reference_gain: float32 [3584], replicated, may hold values from 0.5 to 1.5
- policy_embedding: bfloat16 [131072, 3584], P(('dp', 'mp')), may hold values from -1 to 1
- reference_embedding: bfloat16 [131072, 3584], P(('dp', 'mp')), may hold values from -1 to 1
- mixture_weight: float32 [256], replicated, may hold values from 0.1 to 0.9
- sampled_tokens: int32 [256], replicated, may hold values from 0 to 131071
Outputs:
- mixture_shift: float32 [256, 131072], P(None, ('dp', 'mp'))
- sampled_logprobs: float32 [3, 256], P(None, 'dp')
All inputs are finite; a program needn't handle non-finite values.
Results may differ from a plain program's by a relative error of at most 0.002.
Values may be sent and summed in bfloat16 or wider, within the bound.
A program may use at most 128 MiB of HBM per device.

v0:
```python
import functools

import jax
import jax.numpy as jnp
from jax import lax
from jax.experimental import pallas as pl
from jax.experimental.pallas import tpu as pltpu
from jax.sharding import PartitionSpec as P

softcap = 30.0
epsilon = 1e-06
LANES = 128
TILE = 512
SLOT_BYTES = 40 * 2**20
MESH = pl.DeviceIdType.MESH


def lane_sum(x):
    total = x[:, :LANES]
    for k in range(1, x.shape[1] // LANES):
        total = total + x[:, k * LANES : (k + 1) * LANES]
    return total


def spread(row, lanes):
    return jnp.transpose(jnp.broadcast_to(row, (LANES, row.shape[1])))[:, :lanes]


def kernel(
    n_dp,
    n_mp,
    tile,
    slots,
    ph_hbm,
    rh_hbm,
    pg_hbm,
    rg_hbm,
    pe_hbm,
    re_hbm,
    weight_ref,
    token_ref,
    diff_hbm,
    delta_ref,
    logp_ref,
    hidden,
    gains,
    normed,
    emb,
    diff,
    sums,
    weight_col,
    token_col,
    part_mp,
    part_dp,
    in_sem,
    emb_sem,
    out_sem,
    send_sem,
    recv_sem,
    fsend_sem,
    frecv_sem,
    psend_sem,
    precv_sem,
    msend_sem,
    mrecv_sem,
    dsend_sem,
    drecv_sem,
):
    dp = lax.axis_index("dp")
    mp = lax.axis_index("mp")
    half = lax.rem(mp, 2)
    seq = hidden.shape[1]
    group = 2 * (seq // 16)
    width = hidden.shape[2] // 2
    me = lax.rem(mp, group)
    base = mp - me
    twin = me + 1 - 2 * half
    hops = range(2, group, 2)
    batch = normed.shape[1]
    vocab = pe_hbm.shape[0]
    tiles = vocab // tile

    loads = [
        pltpu.make_async_copy(ph_hbm, hidden.at[0], in_sem.at[0]),
        pltpu.make_async_copy(pg_hbm, gains.at[0], in_sem.at[1]),
        pltpu.make_async_copy(rh_hbm, hidden.at[1], in_sem.at[2]),
        pltpu.make_async_copy(rg_hbm, gains.at[1], in_sem.at[3]),
    ]
    for load in loads:
        load.start()

    def fetch(source, t, slot):
        return pltpu.make_async_copy(
            source.at[pl.ds(pl.multiple_of(t * tile, tile), tile)], emb.at[slot], emb_sem.at[slot]
        )

    for g in range(slots):
        fetch(pe_hbm if g < tiles else re_hbm, g % tiles, g).start()

    barrier = pltpu.get_barrier_semaphore()
    for o in range(1, n_dp):
        pl.semaphore_signal(
            barrier, inc=1, device_id={"dp": lax.rem(dp + o, n_dp)}, device_id_type=MESH
        )
    for o in range(1, n_mp):
        pl.semaphore_signal(
            barrier, inc=1, device_id={"mp": lax.rem(mp + o, n_mp)}, device_id_type=MESH
        )

    def normalize(model):
        loads[2 * model].wait()
        loads[2 * model + 1].wait()
        for r in range(0, seq, 16):
            values = hidden[model, r : r + 16].astype(jnp.float32)
            meansq = jnp.mean(values * values, axis=-1, keepdims=True)
            result = (values * lax.rsqrt(meansq + epsilon) * gains[model]).astype(jnp.bfloat16)
            normed[model, pl.ds(pl.multiple_of(dp * seq + r, 16), 16)] = result

    def block(model, owner, member):
        row = pl.multiple_of(owner * seq + member // 2 * 16, 16)
        column = pl.multiple_of(lax.rem(member, 2) * width, 128)
        return normed.at[model, pl.ds(row, 16), pl.ds(column, width)]

    offsets = sorted(range(1, n_dp), key=lambda o: min(o, n_dp - o))

    def gather_copy(model, o):
        return pltpu.make_async_remote_copy(
            src_ref=block(model, dp, me),
            dst_ref=block(model, dp, me),
            send_sem=send_sem.at[model, o],
            recv_sem=recv_sem.at[model, o],
            device_id={"dp": lax.rem(dp + o, n_dp)},
            device_id_type=MESH,
        )

    def arrived(model, o):
        owner = lax.rem(dp + n_dp - o, n_dp)
        return pltpu.make_async_remote_copy(
            src_ref=block(model, owner, me),
            dst_ref=block(model, owner, me),
            send_sem=send_sem.at[model, o],
            recv_sem=recv_sem.at[model, o],
            device_id={"dp": lax.rem(dp + o, n_dp)},
            device_id_type=MESH,
        )

    def member_of(index, q):
        return lax.rem(index + group - q, group)

    def pass_on(model, o, q, member):
        owner = lax.rem(dp + n_dp - o, n_dp)
        return pltpu.make_async_remote_copy(
            src_ref=block(model, owner, member),
            dst_ref=block(model, owner, member),
            send_sem=psend_sem.at[model, o, q],
            recv_sem=precv_sem.at[model, o, q],
            device_id={"mp": base + lax.rem(me + q, group)},
            device_id_type=MESH,
        )

    def forward(model, o, q, member):
        owner = lax.rem(dp + n_dp - o, n_dp)
        return pltpu.make_async_remote_copy(
            src_ref=block(model, owner, member),
            dst_ref=block(model, owner, member),
            send_sem=fsend_sem.at[model, o, q],
            recv_sem=frecv_sem.at[model, o, q],
            device_id={"mp": base + twin},
            device_id_type=MESH,
        )

    normalize(0)
    pl.semaphore_wait(barrier, n_dp - 1 + n_mp - 1)
    for o in offsets:
        gather_copy(0, o).start()
    normalize(1)
    for o in offsets:
        gather_copy(1, o).start()

    first = (dp * n_mp + mp) * vocab
    weight = weight_ref[...]
    weight_col[...] = spread(weight, LANES)
    local_token = jnp.clip(token_ref[...] - first, -1, vocab).astype(jnp.float32)
    token_col[...] = spread(local_token, LANES)
    sums[...] = jnp.zeros_like(sums)

    def relay(model):
        for o in offsets:
            arrived(model, o).wait_recv()
            for q in hops:
                pass_on(model, o, q, me).start()
            forward(model, o, 0, me).start()
        for o in offsets:
            for q in hops:
                member = member_of(me, q)
                pass_on(model, o, q, member).wait_recv()
                forward(model, o, q, member).start()

    def relayed(model):
        for o in offsets:
            for q in range(0, group, 2):
                forward(model, o, q, member_of(twin, q)).wait_recv()

    def project(model, slot):
        raw = lax.dot_general(
            normed[model],
            emb[slot],
            (((1,), (1,)), ((), ())),
            preferred_element_type=jnp.float32,
        )
        return softcap * jnp.tanh(raw * (1.0 / softcap))

    def picked(t, values):
        total = None
        lane = lax.broadcasted_iota(jnp.int32, (batch, LANES), 1)
        token = token_col[...]
        for k in range(tile // LANES):
            column = (lane + (t * tile + k * LANES)).astype(jnp.float32)
            piece = jnp.where(token == column, values[:, k * LANES : (k + 1) * LANES], 0.0)
            total = piece if total is None else total + piece
        return total

    def columns(t):
        return pl.ds(pl.multiple_of(t * tile, tile), tile)

    relay(0)
    relayed(0)

    @pl.loop(0, tiles)
    def _(t):
        slot = lax.rem(t, slots)
        fetch(pe_hbm, t, slot).wait()
        capped = project(0, slot)
        diff[:, columns(t)] = capped
        sums[0] += lane_sum(jnp.exp(capped))
        sums[3] += picked(t, capped)
        later = t + slots

        @pl.when(later < tiles)
        def _():
            fetch(pe_hbm, later, slot).start()

        @pl.when(jnp.logical_and(later >= tiles, later < 2 * tiles))
        def _():
            fetch(re_hbm, later - tiles, slot).start()

    relay(1)
    relayed(1)

    def put(t):
        return pltpu.make_async_copy(diff.at[:, columns(t)], diff_hbm.at[:, columns(t)], out_sem.at[t])

    @pl.loop(0, tiles)
    def _(t):
        g = t + tiles
        slot = lax.rem(g, slots)
        fetch(re_hbm, t, slot).wait()
        capped = project(1, slot)
        policy = diff[:, columns(t)]
        w = jnp.concatenate([weight_col[...]] * (tile // LANES), axis=1)
        mixed = (1.0 - w) * policy + w * capped
        diff[:, columns(t)] = mixed - policy
        put(t).start()
        sums[1] += lane_sum(jnp.exp(capped))
        sums[2] += lane_sum(jnp.exp(mixed))
        sums[4] += picked(t, capped)
        later = g + slots

        @pl.when(later < 2 * tiles)
        def _():
            fetch(re_hbm, later - tiles, slot).start()

    lane = lax.broadcasted_iota(jnp.int32, (batch, LANES), 1)
    packed = jnp.zeros((batch, LANES), jnp.float32)
    for k in range(5):
        packed = jnp.where(lane == k, jnp.sum(sums[k], axis=1, keepdims=True), packed)
    part_mp[0] = jnp.transpose(packed)[:8]

    def share(buffer, axis, me, n, o, send, recv):
        return pltpu.make_async_remote_copy(
            src_ref=buffer.at[0],
            dst_ref=buffer.at[o],
            send_sem=send.at[o],
            recv_sem=recv.at[o],
            device_id={axis: lax.rem(me + o, n)},
            device_id_type=MESH,
        )

    def reduce(buffer, axis, me, n, send, recv):
        for o in range(1, n):
            share(buffer, axis, me, n, o, send, recv).start()
        for o in range(1, n):
            share(buffer, axis, me, n, o, send, recv).wait_recv()
        total = buffer[0]
        for o in range(1, n):
            total = total + buffer[o]
        return total

    part_dp[0] = reduce(part_mp, "mp", mp, n_mp, msend_sem, mrecv_sem)
    total = reduce(part_dp, "dp", dp, n_dp, dsend_sem, drecv_sem)
    policy_total = jnp.log(total[0:1])
    reference_total = jnp.log(total[1:2])
    mixture_total = jnp.log(total[2:3])
    policy_pick = total[3:4]
    reference_pick = total[4:5]
    mixed_pick = (1.0 - weight) * policy_pick + weight * reference_pick
    logp = (policy_pick - policy_total, reference_pick - reference_total, mixed_pick - mixture_total)
    for k, row in enumerate(logp):
        mine = row[:, :seq]
        for owner in range(1, n_dp):
            mine = jnp.where(dp == owner, row[:, owner * seq : (owner + 1) * seq], mine)
        logp_ref[k : k + 1] = mine
    delta_ref[...] = spread(mixture_total - policy_total, LANES)

    @pl.loop(0, tiles)
    def _(t):
        put(t).wait()

    for model in range(2):
        for o in offsets:
            gather_copy(model, o).wait_send()
            for q in hops:
                pass_on(model, o, q, me).wait_send()
            for q in range(0, group, 2):
                forward(model, o, q, member_of(me, q)).wait_send()
    for o in range(1, n_mp):
        share(part_mp, "mp", mp, n_mp, o, msend_sem, mrecv_sem).wait_send()
    for o in range(1, n_dp):
        share(part_dp, "dp", dp, n_dp, o, dsend_sem, drecv_sem).wait_send()


def local(
    n_dp,
    n_mp,
    policy_hidden,
    reference_hidden,
    policy_gain,
    reference_gain,
    policy_embedding,
    reference_embedding,
    mixture_weight,
    sampled_tokens,
):
    seq, width = policy_hidden.shape
    vocab = policy_embedding.shape[0]
    batch = mixture_weight.shape[0]
    tile = min(TILE, vocab)
    tiles = vocab // tile
    slots = min(2 * tiles, SLOT_BYTES // (tile * width * 2))
    group = 2 * (seq // 16)
    anywhere = pl.BlockSpec(memory_space=pl.ANY)
    vmem = pl.BlockSpec(memory_space=pltpu.VMEM)
    dma = pltpu.SemaphoreType.DMA
    diff, delta, logp = pl.pallas_call(
        functools.partial(kernel, n_dp, n_mp, tile, slots),
        name="mixture",
        out_shape=(
            jax.ShapeDtypeStruct((batch, vocab), jnp.float32),
            jax.ShapeDtypeStruct((batch, LANES), jnp.float32),
            jax.ShapeDtypeStruct((3, seq), jnp.float32),
        ),
        in_specs=[anywhere] * 6 + [vmem] * 2,
        out_specs=(anywhere, vmem, vmem),
        scratch_shapes=[
            pltpu.VMEM((2, seq, width), jnp.bfloat16),
            pltpu.VMEM((2, 1, width), jnp.float32),
            pltpu.VMEM((2, batch, width), jnp.bfloat16),
            pltpu.VMEM((slots, tile, width), jnp.bfloat16),
            pltpu.VMEM((batch, vocab), jnp.float32),
            pltpu.VMEM((5, batch, LANES), jnp.float32),
            pltpu.VMEM((batch, LANES), jnp.float32),
            pltpu.VMEM((batch, LANES), jnp.float32),
            pltpu.VMEM((n_mp, 8, batch), jnp.float32),
            pltpu.VMEM((n_dp, 8, batch), jnp.float32),
            dma((4,)),
            dma((slots,)),
            dma((tiles,)),
            dma((2, n_dp)),
            dma((2, n_dp)),
            dma((2, n_dp, group)),
            dma((2, n_dp, group)),
            dma((2, n_dp, group)),
            dma((2, n_dp, group)),
            dma((n_mp,)),
            dma((n_mp,)),
            dma((n_dp,)),
            dma((n_dp,)),
        ],
        compiler_params=pltpu.CompilerParams(
            collective_id=0, has_side_effects=True, vmem_limit_bytes=57 * 2**20
        ),
    )(
        policy_hidden,
        reference_hidden,
        policy_gain.reshape(1, width),
        reference_gain.reshape(1, width),
        policy_embedding,
        reference_embedding,
        mixture_weight.reshape(1, batch),
        sampled_tokens.reshape(1, batch),
    )
    mixture_shift = diff - delta[:, :1]
    return (mixture_shift, logp)


def solution(mesh):
    in_specs = (
        P("dp", None),
        P("dp", None),
        P(),
        P(),
        P(("dp", "mp"), None),
        P(("dp", "mp"), None),
        P(),
        P(),
    )
    out_specs = (P(None, ("dp", "mp")), P(None, "dp"))
    body = functools.partial(local, mesh.shape["dp"], mesh.shape["mp"])
    return jax.shard_map(body, mesh=mesh, in_specs=in_specs, out_specs=out_specs, check_vma=False)
```

profile of v0, /device:TPU:0, one launch (start us, length us, event | category | flops | bytes accessed | tf_op | source)
XLA Modules:
  0.0 79.6 jit_solution(13979478070994967393)
XLA Ops:
  0.6 1.3 %reshape.16.pg_hbm = f32[1,3584]{1,0:T(1,128)} reshape(f32[3584]{0:T(1024)} %param.10) | data formatting | bytes 28672 | tf_op jit(solution)/shard_map/reshape | solution.py:395
  2.0 1.3 %reshape.17.rg_hbm = f32[1,3584]{1,0:T(1,128)} reshape(f32[3584]{0:T(1024)} %param.11) | data formatting | bytes 28672 | tf_op jit(solution)/shard_map/reshape | solution.py:396
  3.3 69.9 %mixture.1 = (f32[256,4096]{1,0:T(8,128)}, f32[256,128]{1,0:T(8,128)}, f32[3,64]{1,0:T(4,128)}) custom-call(bf16[64,3584]{1,0:T(8,128)(2,1)} %ph_hbm.1, bf16[64,3584]{1,0:T(8,128)(2,1)} %rh_hbm.1, f32[1,3584]{1,0:T(1,128)} %reshape.16.pg_hbm, f32[1,3584]{1,0:T(1,128)} %reshape.17.rg_hbm, bf16[4096,3584]{1,0:T(8,128)(2,1)} %pe_hbm.1, ...), custom_call_target="tpu_custom_call" | custom-call | tf_op jit(solution)/shard_map/mixture/pallas_call | solution.py:354
  73.2 1.0 %slice_reduce_fusion = f32[256]{0:T(256)S(1)} fusion(f32[256,128]{1,0:T(8,128)} %get-tuple-element.6), kind=kLoop, calls=%fused_computation.1 | loop fusion | bytes 2048 | tf_op jit(solution)/shard_map/slice | solution.py:402
  74.2 0.0 copy-start
  74.2 4.8 %broadcast_subtract_fusion = f32[256,4096]{1,0:T(8,128)} fusion(f32[256,4096]{1,0:T(8,128)} %get-tuple-element.5, f32[256]{0:T(256)S(1)} %slice_reduce_fusion), kind=kLoop, calls=%fused_computation | loop fusion | flops 1048576 | bytes 8389632 | tf_op jit(solution)/shard_map/sub | solution.py:402
  79.0 0.0 copy-done
  79.0 0.6 copy.11
Async XLA Ops:
  74.2 4.8 %copy-start = (f32[3,64]{1,0:T(4,128)S(1)}, f32[3,64]{1,0:T(4,128)}, u32[]{:S(2)}) copy-start(f32[3,64]{1,0:T(4,128)} %get-tuple-element.11) | copy-start | bytes 2308
where the time goes:
time: 80 us; the launch traced here: 79.6 us
  Pallas kernels  69.9 us (87%)
  other arithmetic  4.79 us (6%)
  local copies, waits for them, and re-layouts  4.24 us (5%)
    pallas_call x1, Pallas kernels, local(): pl.pallas_call(functools.partial(kernel, n_dp, n_mp, tile, slots), name='...  69.9 us
    sub x1, other arithmetic, local(): mixture_shift = diff - delta[:, :1]  4.79 us

commit v1 on v0

v1 whole, which is shorter than its diff:
```python
import functools

import jax
import jax.numpy as jnp
from jax import lax
from jax.experimental import pallas as pl
from jax.experimental.pallas import tpu as pltpu
from jax.sharding import PartitionSpec as P

softcap = 30.0
epsilon = 1e-06
LANES = 128
LOG2E = 1.4426950408889634
TILE = 512
SLOT_BYTES = 40 * 2**20
ROWS = 32
POLICY_PARTS = (2, 4, 4, 4)
REFERENCE_PARTS = (7, 7)
MESH = pl.DeviceIdType.MESH


def lane_sum(x):
    total = x[:, :LANES]
    for k in range(1, x.shape[1] // LANES):
        total = total + x[:, k * LANES : (k + 1) * LANES]
    return total


def spread(row, lanes):
    return jnp.transpose(jnp.broadcast_to(row, (LANES, row.shape[1])))[:, :lanes]


def kernel(
    n_dp,
    n_mp,
    tile,
    slots,
    chunks,
    ph_hbm,
    rh_hbm,
    pg_hbm,
    rg_hbm,
    pe_hbm,
    re_hbm,
    weight_ref,
    token_ref,
    diff,
    delta_ref,
    logp_ref,
    hidden,
    policy_gain,
    reference_gain,
    normed,
    emb,
    accum,
    sums,
    weight_col,
    token_col,
    part_mp,
    part_dp,
    in_sem,
    emb_sem,
    send_sem,
    recv_sem,
    fsend_sem,
    frecv_sem,
    psend_sem,
    precv_sem,
    msend_sem,
    mrecv_sem,
    dsend_sem,
    drecv_sem,
):
    dp = lax.axis_index("dp")
    mp = lax.axis_index("mp")
    seq = hidden.shape[1]
    blocks = seq // 16
    group = 2 * blocks
    me = lax.rem(mp, group)
    base = mp - me
    half = lax.rem(me, 2)
    twin = me + 1 - 2 * half
    hops = range(2, group, 2)
    batch = normed.shape[1]
    vocab = pe_hbm.shape[0]
    tiles = vocab // tile
    models = range(2)
    steps = [(model, c) for model in models for c in range(len(chunks[model]))]
    gains = (policy_gain, reference_gain)

    own = pl.multiple_of(me // 2 * 16, 16)
    sources = ((ph_hbm, pg_hbm), (rh_hbm, rg_hbm))
    loads = []
    for model, (states, gain) in enumerate(sources):
        loads.append(pltpu.make_async_copy(states, hidden.at[model], in_sem.at[model, 0]))
        loads.append(pltpu.make_async_copy(gain, gains[model], in_sem.at[model, 1]))
    for load in loads:
        load.start()

    def fetch(source, t, slot):
        return pltpu.make_async_copy(
            source.at[pl.ds(t * tile, tile)], emb.at[slot], emb_sem.at[slot]
        )

    for g in range(slots):
        fetch(pe_hbm if g < tiles else re_hbm, g % tiles, g).start(priority=1)

    barrier = pltpu.get_barrier_semaphore()
    for o in range(1, n_dp):
        pl.semaphore_signal(
            barrier, inc=1, device_id={"dp": lax.rem(dp + o, n_dp)}, device_id_type=MESH
        )
    for o in range(1, n_mp):
        pl.semaphore_signal(
            barrier, inc=1, device_id={"mp": lax.rem(mp + o, n_mp)}, device_id_type=MESH
        )

    def normalize(model, row):
        row = pl.multiple_of(row, 16)
        values = hidden[model, pl.ds(row, 16)].astype(jnp.float32)
        meansq = jnp.mean(values * values, axis=-1, keepdims=True)
        gain = gains[model][...].reshape(1, values.shape[1])
        result = (values * lax.rsqrt(meansq + epsilon) * gain).astype(jnp.bfloat16)
        normed[model, pl.ds(pl.multiple_of(dp * seq + row, 16), 16)] = result

    def block(model, c, owner, member):
        start, width = chunks[model][c]
        row = pl.multiple_of(owner * seq + member // 2 * 16, 16)
        column = pl.multiple_of(start + lax.rem(member, 2) * (width // 2), 128)
        return normed.at[model, pl.ds(row, 16), pl.ds(column, width // 2)]

    offsets = sorted(range(1, n_dp), key=lambda o: min(o, n_dp - o))

    def owner_of(o):
        return lax.rem(dp + n_dp - o, n_dp)

    def gather_copy(model, c, o, owner):
        return pltpu.make_async_remote_copy(
            src_ref=block(model, c, owner, me),
            dst_ref=block(model, c, owner, me),
            send_sem=send_sem.at[model, c, o],
            recv_sem=recv_sem.at[model, c, o],
            device_id={"dp": lax.rem(dp + o, n_dp)},
            device_id_type=MESH,
        )

    def member_of(index, q):
        return lax.rem(index + group - q, group)

    def pass_on(model, c, o, q, member):
        return pltpu.make_async_remote_copy(
            src_ref=block(model, c, owner_of(o), member),
            dst_ref=block(model, c, owner_of(o), member),
            send_sem=psend_sem.at[model, c, o, q // 2],
            recv_sem=precv_sem.at[model, c, o, q // 2],
            device_id={"mp": base + lax.rem(me + q, group)},
            device_id_type=MESH,
        )

    def forward(model, c, o, q, member):
        return pltpu.make_async_remote_copy(
            src_ref=block(model, c, owner_of(o), member),
            dst_ref=block(model, c, owner_of(o), member),
            send_sem=fsend_sem.at[model, c, o, q // 2],
            recv_sem=frecv_sem.at[model, c, o, q // 2],
            device_id={"mp": base + twin},
            device_id_type=MESH,
        )

    def stage_a(model, c):
        for o in offsets:
            gather_copy(model, c, o, owner_of(o)).wait_recv()
            for q in hops:
                pass_on(model, c, o, q, me).start()
            forward(model, c, o, 0, me).start()

    def stage_b(model, c):
        for o in offsets:
            for q in hops:
                member = member_of(me, q)
                pass_on(model, c, o, q, member).wait_recv()
                forward(model, c, o, q, member).start()

    def stage_c(model, c):
        for o in offsets:
            for q in range(0, group, 2):
                forward(model, c, o, q, member_of(twin, q)).wait_recv()

    with jax.named_scope("p01_load"):
        loads[0].wait()
        loads[1].wait()
    normalize(0, own)
    with jax.named_scope("p02_barrier"):
        pl.semaphore_wait(barrier, n_dp - 1 + n_mp - 1)
    for c in range(len(chunks[0])):
        for o in offsets:
            gather_copy(0, c, o, dp).start()
    loads[2].wait()
    loads[3].wait()
    normalize(1, own)
    for c in range(len(chunks[1])):
        for o in offsets:
            gather_copy(1, c, o, dp).start()
    with jax.named_scope("p03_norm"):
        for model in models:
            for b in range(1, blocks):
                normalize(model, lax.rem(me // 2 + b, blocks) * 16)

    first = (dp * n_mp + mp) * vocab
    weight = weight_ref[...]
    weight_col[...] = spread(weight, LANES)
    local_token = token_ref[...] - first
    token_col[...] = spread(local_token, LANES)
    sums[...] = jnp.zeros_like(sums)

    def dot(model, c, slot, span):
        start, width = span
        return lax.dot_general(
            normed[model, :, start : start + width],
            emb[slot, :, start : start + width],
            (((1,), (1,)), ((), ())),
            preferred_element_type=jnp.float32,
        )

    def cap(raw):
        return jnp.tanh(raw * (1.0 / softcap))

    def exp_of(share):
        return jnp.exp2(share * (softcap * LOG2E))

    def columns(t):
        return pl.ds(t * tile, tile)

    def arrive(model, t):
        g = model * tiles + t
        fetch(re_hbm if model else pe_hbm, t, g % slots).wait()

    def refill(model, t):
        g = model * tiles + t
        later = g + slots
        if later < 2 * tiles:
            fetch(pe_hbm if later < tiles else re_hbm, later % tiles, g % slots).start(priority=1)

    def policy_end(t, raw):
        capped = cap(raw)
        diff[:, columns(t)] = capped
        sums[0] += lane_sum(exp_of(capped))

    def reference_end(t, raw):
        capped = cap(raw)
        policy = diff[:, columns(t)]
        w = jnp.concatenate([weight_col[...]] * (tile // LANES), axis=1)
        moved = w * (capped - policy)
        diff[:, columns(t)] = moved
        sums[1] += lane_sum(exp_of(capped))
        sums[2] += lane_sum(exp_of(policy + moved))
        lane = lax.broadcasted_iota(jnp.int32, (batch, LANES), 1)
        token = token_col[...] - (t * tile)
        policy_pick = sums[3]
        reference_pick = sums[4]
        for k in range(tile // LANES):
            hit = token == lane + k * LANES
            part = slice(k * LANES, (k + 1) * LANES)
            policy_pick = jnp.where(hit, policy[:, part], policy_pick)
            reference_pick = jnp.where(hit, capped[:, part], reference_pick)
        sums[3] = policy_pick
        sums[4] = reference_pick

    ends = (policy_end, reference_end)
    totals = (diff, accum)

    def compute(model, c, low, high):
        last = c == len(chunks[model]) - 1
        total = totals[model]
        spans = range(low, high)
        if c == 0:
            for t in spans:
                arrive(model, t)
        for t in spans:
            raw = dot(model, c, (model * tiles + t) % slots, chunks[model][c])
            if c > 0:
                raw = total[:, columns(t)] + raw
            if last:
                ends[model](t, raw)
            else:
                total[:, columns(t)] = raw
        if last:
            for t in spans:
                refill(model, t)

    count = len(steps)
    middle = tiles // 2

    def stage(run, index):
        if index < count:
            run(*steps[index])

    with jax.named_scope("p04_first"):
        stage(stage_a, 0)
        stage(stage_a, 1)
        stage(stage_a, 2)
        stage(stage_b, 0)
        stage(stage_c, 0)
    for index, (model, c) in enumerate(steps):
        if middle:
            with jax.named_scope(f"p1{index}_compute_a"):
                compute(model, c, 0, middle)
        if index:
            with jax.named_scope(f"p1{index}_service_b"):
                stage(stage_a, index + 3)
                stage(stage_b, index + 1)
        with jax.named_scope(f"p1{index}_compute_c"):
            compute(model, c, middle, tiles)
        with jax.named_scope(f"p1{index}_service_d"):
            if index == 0:
                stage(stage_a, 3)
                stage(stage_b, 1)
            stage(stage_c, index + 1)

    lane = lax.broadcasted_iota(jnp.int32, (batch, LANES), 1)
    packed = jnp.zeros((batch, LANES), jnp.float32)
    for k in range(5):
        scale = 1.0 if k < 3 else softcap
        packed = jnp.where(lane == k, jnp.sum(sums[k], axis=1, keepdims=True) * scale, packed)
    part_mp[0] = jnp.transpose(packed)[:8]

    def share(buffer, axis, me, n, o, send, recv):
        return pltpu.make_async_remote_copy(
            src_ref=buffer.at[0],
            dst_ref=buffer.at[o],
            send_sem=send.at[o],
            recv_sem=recv.at[o],
            device_id={axis: lax.rem(me + o, n)},
            device_id_type=MESH,
        )

    def begin(buffer, axis, me, n, send, recv):
        for o in range(1, n):
            share(buffer, axis, me, n, o, send, recv).start()

    def finish(buffer, axis, me, n, send, recv):
        for o in range(1, n):
            share(buffer, axis, me, n, o, send, recv).wait_recv()
        total = buffer[0]
        for o in range(1, n):
            total = total + buffer[o]
        return total

    begin(part_mp, "mp", mp, n_mp, msend_sem, mrecv_sem)
    with jax.named_scope("p90_waitsend"):
        for model, c in steps:
            for o in offsets:
                gather_copy(model, c, o, dp).wait_send()
                for q in hops:
                    pass_on(model, c, o, q, me).wait_send()
                for q in range(0, group, 2):
                    forward(model, c, o, q, member_of(me, q)).wait_send()
    with jax.named_scope("p91_redmp"):
        part_dp[0] = finish(part_mp, "mp", mp, n_mp, msend_sem, mrecv_sem)
    begin(part_dp, "dp", dp, n_dp, dsend_sem, drecv_sem)
    for o in range(1, n_mp):
        share(part_mp, "mp", mp, n_mp, o, msend_sem, mrecv_sem).wait_send()
    with jax.named_scope("p92_reddp"):
        total = finish(part_dp, "dp", dp, n_dp, dsend_sem, drecv_sem)
    policy_total = jnp.log(total[0:1])
    reference_total = jnp.log(total[1:2])
    mixture_total = jnp.log(total[2:3])
    policy_pick = total[3:4]
    reference_pick = total[4:5]
    mixed_pick = (1.0 - weight) * policy_pick + weight * reference_pick
    logp = (policy_pick - policy_total, reference_pick - reference_total, mixed_pick - mixture_total)
    for k, row in enumerate(logp):
        mine = row[:, :seq]
        for owner in range(1, n_dp):
            mine = jnp.where(dp == owner, row[:, owner * seq : (owner + 1) * seq], mine)
        logp_ref[k : k + 1] = mine
    delta_ref[...] = spread(mixture_total - policy_total, LANES)
    for o in range(1, n_dp):
        share(part_dp, "dp", dp, n_dp, o, dsend_sem, drecv_sem).wait_send()


def finish_kernel(rows, diff, delta, logp, out_hbm, logp_out, staged, sem):
    copies = []
    for b in range(diff.shape[0] // rows):
        part = slice(b * rows, (b + 1) * rows)
        shift = delta[part, :]
        for k in range(diff.shape[1] // LANES):
            lanes = slice(k * LANES, (k + 1) * LANES)
            staged[part, lanes] = diff[part, lanes] * softcap - shift
        copy = pltpu.make_async_copy(staged.at[part], out_hbm.at[part], sem.at[b])
        copy.start()
        copies.append(copy)
    logp_out[...] = logp[...]
    for copy in copies:
        copy.wait()


def split(width, parts):
    unit = width // sum(parts)
    spans, start = [], 0
    for part in parts:
        spans.append((start, part * unit))
        start += part * unit
    return tuple(spans)


def local(
    n_dp,
    n_mp,
    policy_hidden,
    reference_hidden,
    policy_gain,
    reference_gain,
    policy_embedding,
    reference_embedding,
    mixture_weight,
    sampled_tokens,
):
    seq, width = policy_hidden.shape
    vocab = policy_embedding.shape[0]
    batch = mixture_weight.shape[0]
    tile = min(TILE, vocab)
    tiles = vocab // tile
    slots = min(2 * tiles, SLOT_BYTES // (tile * width * 2))
    assert slots >= tiles
    half = seq // 16
    parts = POLICY_PARTS, REFERENCE_PARTS
    if n_dp > 4:
        parts = (1,), (1,)
    chunks = tuple(split(width, p) for p in parts)
    count = max(len(c) for c in chunks)
    anywhere = pl.BlockSpec(memory_space=pl.ANY)
    vmem = pl.BlockSpec(memory_space=pltpu.VMEM)
    dma = pltpu.SemaphoreType.DMA
    diff, delta, logp = pl.pallas_call(
        functools.partial(kernel, n_dp, n_mp, tile, slots, chunks),
        name="mixture",
        out_shape=(
            pltpu.VMEM((batch, vocab), jnp.float32),
            pltpu.VMEM((batch, LANES), jnp.float32),
            pltpu.VMEM((3, seq), jnp.float32),
        ),
        in_specs=[anywhere] * 6 + [vmem] * 2,
        out_specs=(vmem, vmem, vmem),
        scratch_shapes=[
            pltpu.VMEM((2, seq, width), jnp.bfloat16),
            pltpu.VMEM((width,), jnp.float32),
            pltpu.VMEM((width,), jnp.float32),
            pltpu.VMEM((2, batch, width), jnp.bfloat16),
            pltpu.VMEM((slots, tile, width), jnp.bfloat16),
            pltpu.VMEM((batch, vocab), jnp.float32),
            pltpu.VMEM((5, batch, LANES), jnp.float32),
            pltpu.VMEM((batch, LANES), jnp.float32),
            pltpu.VMEM((batch, LANES), jnp.int32),
            pltpu.VMEM((n_mp, 8, batch), jnp.float32),
            pltpu.VMEM((n_dp, 8, batch), jnp.float32),
            dma((2, 2)),
            dma((slots,)),
            dma((2, count, n_dp)),
            dma((2, count, n_dp)),
            dma((2, count, n_dp, half)),
            dma((2, count, n_dp, half)),
            dma((2, count, n_dp, half)),
            dma((2, count, n_dp, half)),
            dma((n_mp,)),
            dma((n_mp,)),
            dma((n_dp,)),
            dma((n_dp,)),
        ],
        compiler_params=pltpu.CompilerParams(
            collective_id=0, has_side_effects=True, vmem_limit_bytes=54 * 2**20
        ),
    )(
        policy_hidden,
        reference_hidden,
        policy_gain,
        reference_gain,
        policy_embedding,
        reference_embedding,
        mixture_weight.reshape(1, batch),
        sampled_tokens.reshape(1, batch),
    )
    return tuple(
        pl.pallas_call(
            functools.partial(finish_kernel, ROWS),
            name="shift",
            out_shape=(
                jax.ShapeDtypeStruct((batch, vocab), jnp.float32),
                jax.ShapeDtypeStruct((3, seq), jnp.float32),
            ),
            in_specs=[vmem] * 3,
            out_specs=(anywhere, vmem),
            scratch_shapes=[pltpu.VMEM((batch, vocab), jnp.float32), dma((batch // ROWS,))],
            compiler_params=pltpu.CompilerParams(vmem_limit_bytes=12 * 2**20),
        )(*(pltpu.with_memory_space_constraint(x, pltpu.VMEM) for x in (diff, delta, logp)))
    )


def solution(mesh):
    in_specs = (
        P("dp", None),
        P("dp", None),
        P(),
        P(),
        P(("dp", "mp"), None),
        P(("dp", "mp"), None),
        P(),
        P(),
    )
    out_specs = (P(None, ("dp", "mp")), P(None, "dp"))
    body = functools.partial(local, mesh.shape["dp"], mesh.shape["mp"])
    return jax.shard_map(body, mesh=mesh, in_specs=in_specs, out_specs=out_specs, check_vma=False)
```

time: 80 us -> 54.1 us (0.68)
  Pallas kernels: 69.9 us -> 53.1 us
  other arithmetic: 4.79 us -> 0 us
  local copies, waits for them, and re-layouts: 4.24 us -> 0 us
    pallas_call x1 -> x2, Pallas kernels: 69.9 us -> 53.1 us  [the longest x1 50.4 us: local(): pl.pallas_call(functools.partial(kernel, n_dp, n_mp, tile, slots, chunks)...]
    sub x1 -> x0, other arithmetic: 4.79 us -> none  [local(): mixture_shift = diff - delta[:, :1]]
    reshape x2 -> x0, local copies, waits for them, and re-layouts: 2.65 us -> none  [the longest x1 1.33 us: local(): policy_gain.reshape(1, width)]
    slice x1 -> x0, local copies, waits for them, and re-layouts: 1.01 us -> none  [local(): mixture_shift = diff - delta[:, :1]]
where the time goes in v1:
time: 54.1 us; the launch traced here: 53.9 us
  Pallas kernels  53.1 us (98%)
  between operations  0.8 us (1%)
    pallas_call x1, Pallas kernels, local(): pl.pallas_call(functools.partial(kernel, n_dp, n_mp, tile, slots, chunks)...  50.4 us
    pallas_call x1, Pallas kernels, local(): pl.pallas_call(functools.partial(finish_kernel, ROWS), name='shift', out_...  2.69 us

profile of v1, /device:TPU:0, one launch (start us, length us, event | category | flops | bytes accessed | tf_op | source)
XLA Modules:
  0.0 53.9 jit_solution(8032667599106141081)
XLA Ops:
  0.6 50.4 %mixture.1 = (f32[256,4096]{1,0:T(8,128)S(1)}, f32[256,128]{1,0:T(8,128)S(1)}, f32[3,64]{1,0:T(4,128)S(1)}) custom-call(bf16[64,3584]{1,0:T(8,128)(2,1)} %ph_hbm.1, bf16[64,3584]{1,0:T(8,128)(2,1)} %rh_hbm.1, f32[3584]{0:T(1024)} %pg_hbm.1, f32[3584]{0:T(1024)} %rg_hbm.1, bf16[4096,3584]{1,0:T(8,128)(2,1)} %pe_hbm.1, bf16[4096,3584]{1,0:T(8,128)(2,1)} %re_hbm.1, ...), custom_call_target="tpu_custom_call" | custom-call | tf_op jit(solution)/shard_map/mixture/pallas_call | solution.py:435
  51.1 2.7 %shift.1 = (f32[256,4096]{1,0:T(8,128)}, f32[3,64]{1,0:T(4,128)}) custom-call(f32[256,4096]{1,0:T(8,128)S(1)} %get-tuple-element.5.diff, f32[256,128]{1,0:T(8,128)S(1)} %get-tuple-element.6.delta, f32[3,64]{1,0:T(4,128)S(1)} %get-tuple-element.7.logp), custom_call_target="tpu_custom_call" | custom-call | tf_op jit(solution)/shard_map/shift/pallas_call | solution.py:484

commit v2 on v1

--- a/solution.py
+++ b/solution.py
@@ -12,10 +12,12 @@
 LANES = 128
 LOG2E = 1.4426950408889634
 TILE = 512
-SLOT_BYTES = 40 * 2**20
+SLOT_BYTES = 43 * 2**20
 ROWS = 32
+BLOCK = 16
 POLICY_PARTS = (2, 4, 4, 4)
-REFERENCE_PARTS = (7, 7)
+REFERENCE_PARTS = (5, 9)
+CUTS = (6, 8)
 MESH = pl.DeviceIdType.MESH
 
 
@@ -36,6 +38,7 @@
     tile,
     slots,
     chunks,
+    cuts,
     ph_hbm,
     rh_hbm,
     pg_hbm,
@@ -73,7 +76,7 @@
 ):
     dp = lax.axis_index("dp")
     mp = lax.axis_index("mp")
-    seq = hidden.shape[1]
+    seq, width = hidden.shape[1:]
     blocks = seq // 16
     group = 2 * blocks
     me = lax.rem(mp, group)
@@ -97,13 +100,19 @@
     for load in loads:
         load.start()
 
-    def fetch(source, t, slot):
+    def fetch(g, piece):
+        source = re_hbm if g // tiles else pe_hbm
+        start, span = cuts[piece]
         return pltpu.make_async_copy(
-            source.at[pl.ds(t * tile, tile)], emb.at[slot], emb_sem.at[slot]
-        )
-
-    for g in range(slots):
-        fetch(pe_hbm if g < tiles else re_hbm, g % tiles, g).start(priority=1)
+            source.at[pl.ds(g % tiles * tile, tile), pl.ds(start, span)],
+            emb.at[g % slots, :, pl.ds(start, span)],
+            emb_sem.at[g % slots, piece],
+        )
+
+    for held in (range(tiles), range(tiles, slots)):
+        for piece in range(len(cuts)):
+            for g in held:
+                fetch(g, piece).start(priority=1)
 
     barrier = pltpu.get_barrier_semaphore()
     for o in range(1, n_dp):
@@ -124,22 +133,24 @@
         normed[model, pl.ds(pl.multiple_of(dp * seq + row, 16), 16)] = result
 
     def block(model, c, owner, member):
-        start, width = chunks[model][c]
+        start, span = chunks[model][c]
         row = pl.multiple_of(owner * seq + member // 2 * 16, 16)
-        column = pl.multiple_of(start + lax.rem(member, 2) * (width // 2), 128)
-        return normed.at[model, pl.ds(row, 16), pl.ds(column, width // 2)]
+        column = pl.multiple_of(start + lax.rem(member, 2) * (span // 2), 128)
+        return normed.at[model, pl.ds(row, 16), pl.ds(column, span // 2)]
 
     offsets = sorted(range(1, n_dp), key=lambda o: min(o, n_dp - o))
 
     def owner_of(o):
         return lax.rem(dp + n_dp - o, n_dp)
+
+    order = {step: index for index, step in enumerate(steps)}
 
     def gather_copy(model, c, o, owner):
         return pltpu.make_async_remote_copy(
             src_ref=block(model, c, owner, me),
             dst_ref=block(model, c, owner, me),
-            send_sem=send_sem.at[model, c, o],
-            recv_sem=recv_sem.at[model, c, o],
+            send_sem=send_sem.at[model],
+            recv_sem=recv_sem.at[order[model, c], o - 1],
             device_id={"dp": lax.rem(dp + o, n_dp)},
             device_id_type=MESH,
         )
@@ -151,8 +162,8 @@
         return pltpu.make_async_remote_copy(
             src_ref=block(model, c, owner_of(o), member),
             dst_ref=block(model, c, owner_of(o), member),
-            send_sem=psend_sem.at[model, c, o, q // 2],
-            recv_sem=precv_sem.at[model, c, o, q // 2],
+            send_sem=psend_sem.at[model],
+            recv_sem=precv_sem.at[order[model, c]],
             device_id={"mp": base + lax.rem(me + q, group)},
             device_id_type=MESH,
         )
@@ -161,11 +172,17 @@
         return pltpu.make_async_remote_copy(
             src_ref=block(model, c, owner_of(o), member),
             dst_ref=block(model, c, owner_of(o), member),
-            send_sem=fsend_sem.at[model, c, o, q // 2],
-            recv_sem=frecv_sem.at[model, c, o, q // 2],
+            send_sem=fsend_sem.at[model],
+            recv_sem=frecv_sem.at[order[model, c]],
             device_id={"mp": base + twin},
             device_id_type=MESH,
         )
+
+    def drain(model, columns, count, sem):
+        view = normed.at[model, pl.ds(0, 16 * count), pl.ds(0, columns // 2)]
+        pltpu.make_async_copy(view, view, sem).wait()
+
+    peers = n_dp - 1
 
     def stage_a(model, c):
         for o in offsets:
@@ -175,16 +192,13 @@
             forward(model, c, o, 0, me).start()
 
     def stage_b(model, c):
+        drain(model, chunks[model][c][1], peers * (blocks - 1), precv_sem.at[order[model, c]])
         for o in offsets:
             for q in hops:
-                member = member_of(me, q)
-                pass_on(model, c, o, q, member).wait_recv()
-                forward(model, c, o, q, member).start()
+                forward(model, c, o, q, member_of(me, q)).start()
 
     def stage_c(model, c):
-        for o in offsets:
-            for q in range(0, group, 2):
-                forward(model, c, o, q, member_of(twin, q)).wait_recv()
+        drain(model, chunks[model][c][1], peers * blocks, frecv_sem.at[order[model, c]])
 
     with jax.named_scope("p01_load"):
         loads[0].wait()
@@ -214,10 +228,10 @@
     sums[...] = jnp.zeros_like(sums)
 
     def dot(model, c, slot, span):
-        start, width = span
+        part = slice(span[0], sum(span))
         return lax.dot_general(
-            normed[model, :, start : start + width],
-            emb[slot, :, start : start + width],
+            normed[model, :, part],
+            emb[slot, :, part],
             (((1,), (1,)), ((), ())),
             preferred_element_type=jnp.float32,
         )
@@ -231,62 +245,69 @@
     def columns(t):
         return pl.ds(t * tile, tile)
 
-    def arrive(model, t):
-        g = model * tiles + t
-        fetch(re_hbm if model else pe_hbm, t, g % slots).wait()
-
-    def refill(model, t):
-        g = model * tiles + t
-        later = g + slots
-        if later < 2 * tiles:
-            fetch(pe_hbm if later < tiles else re_hbm, later % tiles, g % slots).start(priority=1)
-
-    def policy_end(t, raw):
-        capped = cap(raw)
-        diff[:, columns(t)] = capped
-        sums[0] += lane_sum(exp_of(capped))
-
-    def reference_end(t, raw):
-        capped = cap(raw)
-        policy = diff[:, columns(t)]
-        w = jnp.concatenate([weight_col[...]] * (tile // LANES), axis=1)
-        moved = w * (capped - policy)
-        diff[:, columns(t)] = moved
-        sums[1] += lane_sum(exp_of(capped))
-        sums[2] += lane_sum(exp_of(policy + moved))
-        lane = lax.broadcasted_iota(jnp.int32, (batch, LANES), 1)
-        token = token_col[...] - (t * tile)
-        policy_pick = sums[3]
-        reference_pick = sums[4]
-        for k in range(tile // LANES):
-            hit = token == lane + k * LANES
-            part = slice(k * LANES, (k + 1) * LANES)
-            policy_pick = jnp.where(hit, policy[:, part], policy_pick)
-            reference_pick = jnp.where(hit, capped[:, part], reference_pick)
-        sums[3] = policy_pick
-        sums[4] = reference_pick
+    def arrive(model, c, t):
+        for piece, (start, span) in enumerate(cuts):
+            if chunks[model][c][0] <= start < sum(chunks[model][c]):
+                fetch(model * tiles + t, piece).wait()
+
+    def refill(model, c, t):
+        later = model * tiles + t + slots
+        for piece, (start, span) in enumerate(cuts):
+            if chunks[model][c][0] < start + span <= sum(chunks[model][c]) and later < 2 * tiles:
+                fetch(later, piece).start(priority=1)
+
+    def policy_end(t):
+        for r in range(0, batch, BLOCK):
+            rows = pl.ds(r, BLOCK)
+            capped = cap(diff[rows, columns(t)])
+            diff[rows, columns(t)] = capped
+            sums[0, rows] += lane_sum(exp_of(capped))
+
+    def reference_end(t):
+        lane = lax.broadcasted_iota(jnp.int32, (BLOCK, tile), 1) + t * tile
+        for r in range(0, batch, BLOCK):
+            rows = pl.ds(r, BLOCK)
+            capped = cap(accum[rows, columns(t)])
+            policy = diff[rows, columns(t)]
+            w = jnp.concatenate([weight_col[rows]] * (tile // LANES), axis=1)
+            moved = w * (capped - policy)
+            diff[rows, columns(t)] = moved
+            sums[1, rows] += lane_sum(exp_of(capped))
+            sums[2, rows] += lane_sum(exp_of(policy + moved))
+            token = token_col[rows]
+            policy_pick = sums[3, rows]
+            reference_pick = sums[4, rows]
+            for k in range(tile // LANES):
+                part = slice(k * LANES, (k + 1) * LANES)
+                hit = token == lane[:, part]
+                policy_pick = jnp.where(hit, policy[:, part], policy_pick)
+                reference_pick = jnp.where(hit, capped[:, part], reference_pick)
+            sums[3, rows] = policy_pick
+            sums[4, rows] = reference_pick
 
     ends = (policy_end, reference_end)
     totals = (diff, accum)
+
+    pending = []
+
+    def flush():
+        while pending:
+            model, t = pending.pop()
+            ends[model](t)
 
     def compute(model, c, low, high):
         last = c == len(chunks[model]) - 1
         total = totals[model]
-        spans = range(low, high)
-        if c == 0:
-            for t in spans:
-                arrive(model, t)
-        for t in spans:
+        for t in range(low, high):
             raw = dot(model, c, (model * tiles + t) % slots, chunks[model][c])
             if c > 0:
                 raw = total[:, columns(t)] + raw
+            total[:, columns(t)] = raw
+            flush()
             if last:
-                ends[model](t, raw)
-            else:
-                total[:, columns(t)] = raw
-        if last:
-            for t in spans:
-                refill(model, t)
+                pending.append((model, t))
+        for t in range(low, high):
+            refill(model, c, t)
 
     count = len(steps)
     middle = tiles // 2
@@ -298,24 +319,25 @@
     with jax.named_scope("p04_first"):
         stage(stage_a, 0)
         stage(stage_a, 1)
+        stage(stage_b, 0)
         stage(stage_a, 2)
-        stage(stage_b, 0)
         stage(stage_c, 0)
     for index, (model, c) in enumerate(steps):
+        for t in range(tiles):
+            arrive(model, c, t)
         if middle:
             with jax.named_scope(f"p1{index}_compute_a"):
                 compute(model, c, 0, middle)
-        if index:
-            with jax.named_scope(f"p1{index}_service_b"):
-                stage(stage_a, index + 3)
-                stage(stage_b, index + 1)
+        with jax.named_scope(f"p1{index}_service_b"):
+            if index == 0:
+                stage(stage_a, 3)
+            stage(stage_b, index + 1)
         with jax.named_scope(f"p1{index}_compute_c"):
             compute(model, c, middle, tiles)
         with jax.named_scope(f"p1{index}_service_d"):
-            if index == 0:
-                stage(stage_a, 3)
-                stage(stage_b, 1)
             stage(stage_c, index + 1)
+            stage(stage_a, index + 4)
+    flush()
 
     lane = lax.broadcasted_iota(jnp.int32, (batch, LANES), 1)
     packed = jnp.zeros((batch, LANES), jnp.float32)
@@ -328,19 +350,22 @@
         return pltpu.make_async_remote_copy(
             src_ref=buffer.at[0],
             dst_ref=buffer.at[o],
-            send_sem=send.at[o],
-            recv_sem=recv.at[o],
+            send_sem=send.at[0],
+            recv_sem=recv.at[0],
             device_id={axis: lax.rem(me + o, n)},
             device_id_type=MESH,
         )
+
+    def settle(buffer, n, sem):
+        view = buffer.at[pl.ds(1, n - 1)]
+        pltpu.make_async_copy(view, view, sem.at[0]).wait()
 
     def begin(buffer, axis, me, n, send, recv):
         for o in range(1, n):
             share(buffer, axis, me, n, o, send, recv).start()
 
-    def finish(buffer, axis, me, n, send, recv):
-        for o in range(1, n):
-            share(buffer, axis, me, n, o, send, recv).wait_recv()
+    def finish(buffer, n, recv):
+        settle(buffer, n, recv)
         total = buffer[0]
         for o in range(1, n):
             total = total + buffer[o]
@@ -348,20 +373,16 @@
 
     begin(part_mp, "mp", mp, n_mp, msend_sem, mrecv_sem)
     with jax.named_scope("p90_waitsend"):
-        for model, c in steps:
-            for o in offsets:
-                gather_copy(model, c, o, dp).wait_send()
-                for q in hops:
-                    pass_on(model, c, o, q, me).wait_send()
-                for q in range(0, group, 2):
-                    forward(model, c, o, q, member_of(me, q)).wait_send()
+        for model in models:
+            drain(model, width, peers, send_sem.at[model])
+            drain(model, width, peers * (blocks - 1), psend_sem.at[model])
+            drain(model, width, peers * blocks, fsend_sem.at[model])
     with jax.named_scope("p91_redmp"):
-        part_dp[0] = finish(part_mp, "mp", mp, n_mp, msend_sem, mrecv_sem)
+        part_dp[0] = finish(part_mp, n_mp, mrecv_sem)
     begin(part_dp, "dp", dp, n_dp, dsend_sem, drecv_sem)
-    for o in range(1, n_mp):
-        share(part_mp, "mp", mp, n_mp, o, msend_sem, mrecv_sem).wait_send()
+    settle(part_mp, n_mp, msend_sem)
     with jax.named_scope("p92_reddp"):
-        total = finish(part_dp, "dp", dp, n_dp, dsend_sem, drecv_sem)
+        total = finish(part_dp, n_dp, drecv_sem)
     policy_total = jnp.log(total[0:1])
     reference_total = jnp.log(total[1:2])
     mixture_total = jnp.log(total[2:3])
@@ -375,8 +396,7 @@
             mine = jnp.where(dp == owner, row[:, owner * seq : (owner + 1) * seq], mine)
         logp_ref[k : k + 1] = mine
     delta_ref[...] = spread(mixture_total - policy_total, LANES)
-    for o in range(1, n_dp):
-        share(part_dp, "dp", dp, n_dp, o, dsend_sem, drecv_sem).wait_send()
+    settle(part_dp, n_dp, dsend_sem)
 
 
 def finish_kernel(rows, diff, delta, logp, out_hbm, logp_out, staged, sem):
@@ -423,17 +443,17 @@
     tiles = vocab // tile
     slots = min(2 * tiles, SLOT_BYTES // (tile * width * 2))
     assert slots >= tiles
-    half = seq // 16
     parts = POLICY_PARTS, REFERENCE_PARTS
     if n_dp > 4:
         parts = (1,), (1,)
     chunks = tuple(split(width, p) for p in parts)
-    count = max(len(c) for c in chunks)
+    count = sum(len(c) for c in chunks)
+    cuts = split(width, CUTS if n_dp <= 4 else (1,))
     anywhere = pl.BlockSpec(memory_space=pl.ANY)
     vmem = pl.BlockSpec(memory_space=pltpu.VMEM)
     dma = pltpu.SemaphoreType.DMA
     diff, delta, logp = pl.pallas_call(
-        functools.partial(kernel, n_dp, n_mp, tile, slots, chunks),
+        functools.partial(kernel, n_dp, n_mp, tile, slots, chunks, cuts),
         name="mixture",
         out_shape=(
             pltpu.VMEM((batch, vocab), jnp.float32),
@@ -455,17 +475,17 @@
             pltpu.VMEM((n_mp, 8, batch), jnp.float32),
             pltpu.VMEM((n_dp, 8, batch), jnp.float32),
             dma((2, 2)),
-            dma((slots,)),
-            dma((2, count, n_dp)),
-            dma((2, count, n_dp)),
-            dma((2, count, n_dp, half)),
-            dma((2, count, n_dp, half)),
-            dma((2, count, n_dp, half)),
-            dma((2, count, n_dp, half)),
-            dma((n_mp,)),
-            dma((n_mp,)),
-            dma((n_dp,)),
-            dma((n_dp,)),
+            dma((slots, len(cuts))),
+            dma((2,)),
+            dma((count, n_dp - 1)),
+            dma((2,)),
+            dma((count,)),
+            dma((2,)),
+            dma((count,)),
+            dma((1,)),
+            dma((1,)),
+            dma((1,)),
+            dma((1,)),
         ],
         compiler_params=pltpu.CompilerParams(
             collective_id=0, has_side_effects=True, vmem_limit_bytes=54 * 2**20

time: 54.1 us -> 46.1 us (0.85)
  Pallas kernels: 53.1 us -> 45.1 us
    pallas_call x1, Pallas kernels: 50.4 us -> 42.4 us  [local(): pl.pallas_call(functools.partial(kernel, n_dp, n_mp, tile, slots, chunks,...]
where the time goes in v2:
time: 46.1 us; the launch traced here: 45.9 us
  Pallas kernels  45.1 us (98%)
  between operations  0.8 us (2%)
    pallas_call x1, Pallas kernels, local(): pl.pallas_call(functools.partial(kernel, n_dp, n_mp, tile, slots, chunks,...  42.4 us
    pallas_call x1, Pallas kernels, local(): pl.pallas_call(functools.partial(finish_kernel, ROWS), name='shift', out_...  2.69 us

profile of v2, /device:TPU:0, one launch (start us, length us, event | category | flops | bytes accessed | tf_op | source)
XLA Modules:
  0.0 45.9 jit_solution(1512188773692516657)
XLA Ops:
  0.6 42.4 %mixture.1 = (f32[256,4096]{1,0:T(8,128)S(1)}, f32[256,128]{1,0:T(8,128)S(1)}, f32[3,64]{1,0:T(4,128)S(1)}) custom-call(bf16[64,3584]{1,0:T(8,128)(2,1)} %ph_hbm.1, bf16[64,3584]{1,0:T(8,128)(2,1)} %rh_hbm.1, f32[3584]{0:T(1024)} %pg_hbm.1, f32[3584]{0:T(1024)} %rg_hbm.1, bf16[4096,3584]{1,0:T(8,128)(2,1)} %pe_hbm.1, bf16[4096,3584]{1,0:T(8,128)(2,1)} %re_hbm.1, ...), custom_call_target="tpu_custom_call" | custom-call | tf_op jit(solution)/shard_map/mixture/pallas_call | solution.py:455
  43.1 2.7 %shift.1 = (f32[256,4096]{1,0:T(8,128)}, f32[3,64]{1,0:T(4,128)}) custom-call(f32[256,4096]{1,0:T(8,128)S(1)} %get-tuple-element.5.diff, f32[256,128]{1,0:T(8,128)S(1)} %get-tuple-element.6.delta, f32[3,64]{1,0:T(4,128)S(1)} %get-tuple-element.7.logp), custom_call_target="tpu_custom_call" | custom-call | tf_op jit(solution)/shard_map/shift/pallas_call | solution.py:504
